TPU v7x, 32 devices: a whole 2x2x4 slice. The times are simulated.
32 devices in a mesh: silo: 4 (over z), row: 8 (over y, x, core).
Axes of the slice: x: 2, y: 2, z: 4, core: 2. Of those that a mesh axis runs over, the one named last changes fastest.
Arguments:
- silo_grams: float32 [8, 4096, 4096], P('silo', 'row'), may hold values from -9 to 81, as said below
- silo_weights: bfloat16 [8, 4096, 640], P('silo', 'row'), may hold values from -6 to 6
Outputs:
- merged_rows: float32 [640, 4096], P(('silo', 'row'))
Inputs may be any that keep to these rules, and one draw needn't show every extreme that they name: `silo_grams`: each silo's Gram is symmetric up to float32 rounding and positive definite.
All inputs are finite; a program needn't handle non-finite values.
Results may differ from a plain program's by a relative error of at most 0.0003.
Values may be sent and summed in bfloat16 or wider, within the bound.
No kernel may reach another device: no remote copies, remote signals or barrier semaphores. Data moves between devices by JAX's collectives and lax.ppermute only.
A program may use at most 128 MiB of HBM per device.

v0:
```python
import jax
import jax.numpy as jnp
from jax import lax
from jax.sharding import PartitionSpec as P

ITERS = 2
full_precision = lax.Precision.HIGHEST


def conj_grad(right_side, apply_op, sum_squares, sum_curv):
    solution = jnp.zeros_like(right_side)
    residual = right_side
    direction = right_side
    res_norm = sum_squares(jnp.sum(residual * residual, axis=0))
    for iteration in range(ITERS):
        mapped = apply_op(direction)
        step_size = res_norm / sum_curv(jnp.sum(direction * mapped, axis=0))
        solution = solution + step_size * direction
        residual = residual - step_size * mapped
        if iteration + 1 < ITERS:
            next_norm = sum_squares(jnp.sum(residual * residual, axis=0))
            direction = residual + next_norm / res_norm * direction
            res_norm = next_norm
    return solution


def local(silo_grams, silo_weights):
    partial_op = jnp.sum(silo_grams, axis=0)
    partial_rhs = jnp.einsum(
        "srk,skc->rc",
        silo_grams,
        lax.all_gather(silo_weights, "row", axis=1, tiled=True).astype(jnp.float32),
        precision=full_precision,
    )
    operator = lax.psum(partial_op, "silo")
    right_side = lax.psum_scatter(partial_rhs, "silo", scatter_dimension=1, tiled=True)

    def apply_cols(direction):
        return jnp.dot(
            operator, lax.all_gather(direction, "row", axis=0, tiled=True), precision=full_precision
        )

    def squares_cols(values):
        return lax.psum(values, "row")

    def curv_values(values):
        return lax.psum(values, "row")

    solution = conj_grad(right_side, apply_cols, squares_cols, curv_values)
    transposed = solution.T
    return lax.all_to_all(transposed, "row", split_axis=0, concat_axis=1, tiled=True)


def solution(mesh):
    placed = (P("silo", "row", None), P("silo", "row", None))
    return jax.shard_map(
        local, mesh=mesh, in_specs=placed, out_specs=P(("silo", "row"), None), check_vma=False
    )
```

profile of v0, /device:TPU:0, one launch (start us, length us, event | category | flops | bytes accessed | tf_op | source)
XLA Modules:
  0.0 567.5 jit_solution(10931932025676428913)
XLA Ops:
  6.5 2.4 copy.6
  9.0 0.0 reduce-scatter.2.cloned.1.call-start
  9.0 68.1 %all-gather.4.cloned.1.call-done = bf16[2,4096,640]{1,2,0:T(8,128)(2,1)} async-done(((bf16[2,512,640]{1,2,0:T(8,128)(2,1)}), bf16[2,4096,640]{1,2,0:T(8,128)(2,1)}) %all-gather.4.cloned.1.call-update) | async-done | bytes 10485776 | tf_op jit(solution)/shard_map/all_gather | solution.py:32
  77.1 21.3 %convolution_bitcast_fusion = f32[512,640]{0,1:T(8,128)} fusion(f32[2,512,4096]{2,1,0:T(8,128)} %param.2, bf16[2,4096,640]{1,2,0:T(8,128)(2,1)} %all-gather.4.cloned.1.call-done), kind=kOutput, calls=%fused_computation | convolution fusion | flops 32212254720 | bytes 28573696 | tf_op jit(solution)/shard_map/srk,skc->rc/dot_general | solution.py:29
  98.4 0.0 reduce-scatter.2.cloned.1.call-update
  98.5 0.0 all-reduce.3.cloned.1.call-start
  98.5 11.6 %reduce_sum.46 = f32[512,4096]{1,0:T(8,128)} reduce(f32[2,512,4096]{2,1,0:T(8,128)} %param.2, f32[]{:T(128)} %constant.0.clone.1), dimensions={0}, to_apply=%region_3.0 | reduce | flops 2097152 | bytes 25165828 | tf_op jit(solution)/shard_map/reduce_sum | solution.py:28
  110.1 0.0 all-gather.6.cloned.1.call-start
  110.2 19.8 %reduce-scatter.2.cloned.1.call-done = f32[512,160]{0,1:T(8,128)} async-done(((f32[512,640]{0,1:T(8,128)}), f32[512,160]{0,1:T(8,128)}) %reduce-scatter.2.cloned.1.call-update) | async-done | bytes 327696 | tf_op jit(solution)/shard_map/reduce_scatter | solution.py:36
  130.0 0.2 all-gather.8.cloned.1.call-start
  130.2 291.8 %all-reduce.3.cloned.1.call-done = f32[512,4096]{1,0:T(8,128)} async-done(((f32[512,4096]{1,0:T(8,128)}), f32[512,4096]{1,0:T(8,128)}) %all-reduce.3.cloned.1.call-update) | async-done | bytes 8388624 | tf_op jit(solution)/shard_map/psum | solution.py:35
  422.0 30.8 %all-gather.6.cloned.1.call-done = f32[4096,160]{0,1:T(8,128)} async-done(((f32[512,160]{0,1:T(8,128)}), f32[4096,160]{0,1:T(8,128)}) %all-gather.6.cloned.1.call-update) | async-done | bytes 2621456 | tf_op jit(solution)/shard_map/all_gather | solution.py:40
  452.8 13.3 %multiply_reduce_fusion.1 = (f32[160]{0:T(256)S(1)}, f32[160]{0:T(256)S(1)}, f32[512,160]{0,1:T(8,128)S(1)}) fusion(f32[512,160]{0,1:T(8,128)} %reduce-scatter.2.cloned.1.call-done, f32[512,4096]{1,0:T(8,128)} %all-reduce.3.cloned.1.call-done, f32[4096,160]{0,1:T(8,128)} %all-gather.6.cloned.1.call-done), kind=kOutput, calls=%fused_computation.7 | convolution fusion | flops 4026859264 | bytes 11666688 | tf_op jit(solution)/shard_map/dot_general | solution.py:39
  466.0 13.1 %all-reduce = (f32[160]{0:T(256)S(1)}, f32[160]{0:T(256)S(1)}) all-reduce(f32[160]{0:T(256)S(1)} %get-tuple-element.6, f32[160]{0:T(256)S(1)} %get-tuple-element.5), channel_id=1, replica_groups=mesh['silo'=4,'row'=8] {'row'}, use_global_device_ids=true, to_apply=%region_2.0 | all-reduce | flops 320 | bytes 2560 | tf_op jit(solution)/shard_map/psum | solution.py:44
  479.1 0.2 multiply_reduce_fusion
  479.3 12.0 %psum.38 = f32[160]{0:T(256)S(1)} all-reduce(f32[160]{0:T(256)S(1)} %multiply_reduce_fusion), channel_id=1, replica_groups=mesh['silo'=4,'row'=8] {'row'}, use_global_device_ids=true, to_apply=%region_8.0 | all-reduce | flops 160 | bytes 1280 | tf_op jit(solution)/shard_map/psum | solution.py:44
  491.4 0.9 multiply_add_fusion
  492.3 30.1 %all-gather.8.cloned.1.call-done = f32[4096,160]{0,1:T(8,128)} async-done(((f32[512,160]{0,1:T(8,128)}), f32[4096,160]{0,1:T(8,128)}) %all-gather.8.cloned.1.call-update) | async-done | bytes 2621456 | tf_op jit(solution)/shard_map/all_gather | solution.py:40
  522.4 13.2 %fusion = f32[160]{0:T(256)S(1)} fusion(f32[512,160]{0,1:T(8,128)} %multiply_add_fusion, f32[512,4096]{1,0:T(8,128)} %all-reduce.3.cloned.1.call-done, f32[4096,160]{0,1:T(8,128)} %all-gather.8.cloned.1.call-done), kind=kOutput, calls=%fused_computation.2 | convolution fusion | flops 4026695680 | bytes 11338368 | tf_op jit(solution)/shard_map/dot_general | solution.py:39
  535.7 13.1 %psum.39 = f32[160]{0:T(256)S(1)} all-reduce(f32[160]{0:T(256)S(1)} %fusion), channel_id=1, replica_groups=mesh['silo'=4,'row'=8] {'row'}, use_global_device_ids=true, to_apply=%region_10.0 | all-reduce | flops 160 | bytes 1280 | tf_op jit(solution)/shard_map/psum | solution.py:47
  548.8 0.1 add_bitcast_fusion
  548.9 10.9 %all_to_all.19 = f32[8,20,512]{2,1,0:T(8,128)S(1)} all-to-all(f32[8,20,512]{2,1,0:T(8,128)S(1)} %all_to_all.14), channel_id=1, replica_groups=mesh['silo'=4,'row'=8] {'row'}, dimensions={0} | all-to-all | bytes 655360 | tf_op jit(solution)/shard_map/all_to_all | solution.py:51
  559.8 0.2 copy.7
  560.0 1.0 copy.8
  (14 shorter events, 0.2 us)
Async XLA Ops:
  6.5 70.6 %all-gather.4.cloned.1.call-start = ((), (), s32[]{:S(2)}) async-start(), calls=%async_computation.2 | async-start | bytes 11796480 | tf_op jit(solution)/shard_map/all_gather | solution.py:32
  9.0 121.0 %reduce-scatter.2.cloned.1.call-start = ((), (), s32[]{:S(2)}) async-start(), calls=%async_computation.3 | async-start | bytes 1638400 | tf_op jit(solution)/shard_map/reduce_scatter | solution.py:36
  98.5 323.5 %all-reduce.3.cloned.1.call-start = ((), (), s32[]{:S(2)}) async-start(), calls=%async_computation.4 | async-start | bytes 16777216 | tf_op jit(solution)/shard_map/psum | solution.py:35
  110.1 342.7 %all-gather.6.cloned.1.call-start = ((), (), s32[]{:S(2)}) async-start(), calls=%async_computation.5 | async-start | bytes 2949120 | tf_op jit(solution)/shard_map/all_gather | solution.py:40
  130.0 349.2 %copy-start = (f32[512,160]{0,1:T(8,128)S(1)}, f32[512,160]{0,1:T(8,128)}, u32[]{:S(2)}) copy-start(f32[512,160]{0,1:T(8,128)} %reduce-scatter.2.cloned.1.call-done) | copy-start | bytes 983044
  130.0 392.4 %all-gather.8.cloned.1.call-start = ((), (), s32[]{:S(2)}) async-start(), calls=%async_computation.6 | async-start | bytes 2949120 | tf_op jit(solution)/shard_map/all_gather | solution.py:40
  492.2 56.5 %copy-start.1 = (f32[512,160]{0,1:T(8,128)S(1)}, f32[512,160]{0,1:T(8,128)}, u32[]{:S(2)}) copy-start(f32[512,160]{0,1:T(8,128)} %multiply_add_fusion) | copy-start | bytes 983044
Sparse Core Ops, SparseCore 0:
  9.2 67.8 all-gather.3
  98.6 31.3 reduce-scatter.1
  132.5 289.4 all-reduce.2
  423.8 28.9 all-gather.5
  492.4 29.9 all-gather.7
where the time goes:
time: 568 us
  waiting for transfers between devices  441 us (78%)
  blocking collectives  49 us (9%)
  matrix products  47.8 us (8%)
  between operations  13.2 us (2%)
  other arithmetic  12.8 us (2%)
    psum x1, waiting for transfers between devices, local(): operator = lax.psum(partial_op, 'silo')  292 us
    all_gather x1, waiting for transfers between devices, local(): lax.all_gather(silo_weights, 'row', axis=1, tiled=True).astype(jnp.float32)  68.1 us
    all_gather x2, waiting for transfers between devices, apply_cols(): lax.all_gather(direction, 'row', axis=0, tiled=True)  60.9 us
    dot_general x2, matrix products, apply_cols(): jnp.dot(operator, lax.all_gather(direction, 'row', axis=0, tiled=True), p...  26.5 us
    psum x2, blocking collectives, squares_cols(): return lax.psum(values, 'row')  25.1 us
    dot_general x1, matrix products, local(): jnp.einsum('srk,skc->rc', silo_grams, lax.all_gather(silo_weights, 'row',...  21.3 us
    reduce_scatter x1, waiting for transfers between devices, local(): lax.psum_scatter(partial_rhs, 'silo', scatter_dimension=1, tiled=True)  19.8 us
    psum x1, blocking collectives, curv_values(): return lax.psum(values, 'row')  13.1 us
  transfers between devices with their start and end apart: 5, of which 5 were waited for; matrix products, arithmetic and copies ran while one was open for 2% of the time, Pallas kernels for 0%

commit v1 on v0

--- a/solution.py
+++ b/solution.py
@@ -32,7 +32,9 @@
         lax.all_gather(silo_weights, "row", axis=1, tiled=True).astype(jnp.float32),
         precision=full_precision,
     )
-    operator = lax.psum(partial_op, "silo")
+    operator = partial_op
+    for hop in (1, 2):
+        operator = operator + lax.ppermute(operator, "silo", [(dev, dev ^ hop) for dev in range(4)])
     right_side = lax.psum_scatter(partial_rhs, "silo", scatter_dimension=1, tiled=True)
 
     def apply_cols(direction):

time: 568 us -> 725 us (1.28)
  waiting for transfers between devices: 441 us -> 571 us
  other arithmetic: 12.8 us -> 35.8 us
    ppermute x0 -> x2, waiting for transfers between devices: none -> 351 us  [local(): lax.ppermute(operator, 'silo', [(dev, dev ^ hop) for dev in range(4)])]
    psum x1 -> x0, waiting for transfers between devices: 292 us -> none  [local(): operator = lax.psum(partial_op, 'silo')]
    reduce_scatter x1, waiting for transfers between devices: 19.8 us -> 189 us  [local(): lax.psum_scatter(partial_rhs, 'silo', scatter_dimension=1, tiled=True)]
    all_gather x1, waiting for transfers between devices: 68.1 us -> 0.01 us  [local(): lax.all_gather(silo_weights, 'row', axis=1, tiled=True).astype(jnp.float32)]
    all_gather x2, waiting for transfers between devices: 60.9 us -> 30.4 us  [apply_cols(): lax.all_gather(direction, 'row', axis=0, tiled=True)]
    add x0 -> x2, other arithmetic: none -> 22.5 us  [local(): operator + lax.ppermute(operator, 'silo', [(dev, dev ^ hop) for dev in ra...]
  transfers between devices with their start and end apart: 5 -> 6, of which waited for: 5 -> 4; matrix products, arithmetic and copies ran while one was open for 2% -> 8% of each run, Pallas kernels for 0% -> 0%
where the time goes in v1:
time: 725 us
  waiting for transfers between devices  571 us (79%)
  blocking collectives  48.7 us (7%)
  matrix products  46.7 us (6%)
  other arithmetic  35.8 us (5%)
  between operations  13.2 us (2%)
    ppermute x2, waiting for transfers between devices, local(): lax.ppermute(operator, 'silo', [(dev, dev ^ hop) for dev in range(4)])  351 us
    reduce_scatter x1, waiting for transfers between devices, local(): lax.psum_scatter(partial_rhs, 'silo', scatter_dimension=1, tiled=True)  189 us
    all_gather x2, waiting for transfers between devices, apply_cols(): lax.all_gather(direction, 'row', axis=0, tiled=True)  30.4 us
    dot_general x2, matrix products, apply_cols(): jnp.dot(operator, lax.all_gather(direction, 'row', axis=0, tiled=True), p...  25.4 us
    psum x2, blocking collectives, squares_cols(): return lax.psum(values, 'row')  24.8 us
    add x2, other arithmetic, local(): operator + lax.ppermute(operator, 'silo', [(dev, dev ^ hop) for dev in ra...  22.5 us
    dot_general x1, matrix products, local(): jnp.einsum('srk,skc->rc', silo_grams, lax.all_gather(silo_weights, 'row',...  21.3 us
  transfers between devices with their start and end apart: 6, of which 4 were waited for; matrix products, arithmetic and copies ran while one was open for 8% of the time, Pallas kernels for 0%

profile of v1, /device:TPU:0, one launch (start us, length us, event | category | flops | bytes accessed | tf_op | source)
XLA Modules:
  0.0 724.5 jit_solution(16021160868798329673)
XLA Ops:
  6.5 2.4 copy.6
  9.0 0.0 reduce-scatter.2.cloned.1.call-start
  9.0 12.0 %reduce_sum.46 = f32[512,4096]{1,0:T(8,128)} reduce(f32[2,512,4096]{2,1,0:T(8,128)} %param.2, f32[]{:T(128)} %constant.0.clone.1), dimensions={0}, to_apply=%region_3.0 | reduce | flops 2097152 | bytes 25165828 | tf_op jit(solution)/shard_map/reduce_sum | solution.py:28
  21.1 2.8 collective-permute-start
  23.9 180.8 %collective-permute-done = f32[512,4096]{1,0:T(8,128)} collective-permute-done((f32[512,4096]{1,0:T(8,128)}, f32[512,4096]{1,0:T(8,128)}, u32[]{:S(2)}, u32[]{:S(2)}) %collective-permute-start) | collective-permute-done | bytes 8388640 | tf_op jit(solution)/shard_map/ppermute | solution.py:37
  204.7 11.3 %add.22 = f32[512,4096]{1,0:T(8,128)} add(f32[512,4096]{1,0:T(8,128)} %reduce_sum.46, f32[512,4096]{1,0:T(8,128)} %collective-permute-done) | non-fusion elementwise | flops 2097152 | bytes 25165824 | tf_op jit(solution)/shard_map/add | solution.py:37
  216.0 2.7 collective-permute-start.1
  218.7 21.3 %convolution_bitcast_fusion = f32[512,640]{0,1:T(8,128)} fusion(f32[2,512,4096]{2,1,0:T(8,128)} %param.2, bf16[2,4096,640]{1,2,0:T(8,128)(2,1)} %all-gather.4.cloned.1.call-done), kind=kOutput, calls=%fused_computation | convolution fusion | flops 32212254720 | bytes 28573696 | tf_op jit(solution)/shard_map/srk,skc->rc/dot_general | solution.py:29
  240.1 188.8 %reduce-scatter.2.cloned.1.call-done = f32[512,160]{0,1:T(8,128)} async-done(((f32[512,640]{0,1:T(8,128)}), f32[512,160]{0,1:T(8,128)}) %reduce-scatter.2.cloned.1.call-update) | async-done | bytes 327696 | tf_op jit(solution)/shard_map/reduce_scatter | solution.py:38
  429.0 0.2 all-gather.8.cloned.1.call-start
  429.2 170.5 %collective-permute-done.1 = f32[512,4096]{1,0:T(8,128)} collective-permute-done((f32[512,4096]{1,0:T(8,128)}, f32[512,4096]{1,0:T(8,128)}, u32[]{:S(2)}, u32[]{:S(2)}) %collective-permute-start.1) | collective-permute-done | bytes 8388640 | tf_op jit(solution)/shard_map/ppermute | solution.py:37
  599.7 11.3 %add.23 = f32[512,4096]{1,0:T(8,128)} add(f32[512,4096]{1,0:T(8,128)} %add.22, f32[512,4096]{1,0:T(8,128)} %collective-permute-done.1) | non-fusion elementwise | flops 2097152 | bytes 25165824 | tf_op jit(solution)/shard_map/add | solution.py:37
  611.0 12.1 %multiply_reduce_fusion.1 = (f32[160]{0:T(256)S(1)}, f32[160]{0:T(256)S(1)}, f32[512,160]{0,1:T(8,128)S(1)}) fusion(f32[512,160]{0,1:T(8,128)S(1)} %copy-done, f32[512,4096]{1,0:T(8,128)} %add.23, f32[4096,160]{0,1:T(8,128)} %all-gather.6.cloned.1.call-done), kind=kOutput, calls=%fused_computation.7 | convolution fusion | flops 4026859264 | bytes 11666688 | tf_op jit(solution)/shard_map/dot_general | solution.py:41
  623.2 12.8 %all-reduce = (f32[160]{0:T(256)S(1)}, f32[160]{0:T(256)S(1)}) all-reduce(f32[160]{0:T(256)S(1)} %get-tuple-element.6, f32[160]{0:T(256)S(1)} %get-tuple-element.5), channel_id=1, replica_groups=mesh['silo'=4,'row'=8] {'row'}, use_global_device_ids=true, to_apply=%region_2.0 | all-reduce | flops 320 | bytes 2560 | tf_op jit(solution)/shard_map/psum | solution.py:46
  635.9 0.2 multiply_reduce_fusion
  636.1 12.0 %psum.30 = f32[160]{0:T(256)S(1)} all-reduce(f32[160]{0:T(256)S(1)} %multiply_reduce_fusion), channel_id=1, replica_groups=mesh['silo'=4,'row'=8] {'row'}, use_global_device_ids=true, to_apply=%region_7.0 | all-reduce | flops 160 | bytes 1280 | tf_op jit(solution)/shard_map/psum | solution.py:46
  648.1 0.9 multiply_add_fusion
  649.0 30.4 %all-gather.8.cloned.1.call-done = f32[4096,160]{0,1:T(8,128)} async-done(((f32[512,160]{0,1:T(8,128)}), f32[4096,160]{0,1:T(8,128)}) %all-gather.8.cloned.1.call-update) | async-done | bytes 2621456 | tf_op jit(solution)/shard_map/all_gather | solution.py:42
  679.4 13.2 %fusion = f32[160]{0:T(256)S(1)} fusion(f32[512,160]{0,1:T(8,128)} %multiply_add_fusion, f32[512,4096]{1,0:T(8,128)} %add.23, f32[4096,160]{0,1:T(8,128)} %all-gather.8.cloned.1.call-done), kind=kOutput, calls=%fused_computation.2 | convolution fusion | flops 4026695680 | bytes 11338368 | tf_op jit(solution)/shard_map/dot_general | solution.py:41
  692.6 13.1 %psum.31 = f32[160]{0:T(256)S(1)} all-reduce(f32[160]{0:T(256)S(1)} %fusion), channel_id=1, replica_groups=mesh['silo'=4,'row'=8] {'row'}, use_global_device_ids=true, to_apply=%region_9.0 | all-reduce | flops 160 | bytes 1280 | tf_op jit(solution)/shard_map/psum | solution.py:49
  705.7 0.1 add_bitcast_fusion
  705.9 10.9 %all_to_all.19 = f32[8,20,512]{2,1,0:T(8,128)S(1)} all-to-all(f32[8,20,512]{2,1,0:T(8,128)S(1)} %all_to_all.14), channel_id=1, replica_groups=mesh['silo'=4,'row'=8] {'row'}, dimensions={0} | all-to-all | bytes 655360 | tf_op jit(solution)/shard_map/all_to_all | solution.py:53
  716.8 0.2 copy.7
  717.0 1.0 copy.8
  (17 shorter events, 0.2 us)
Async XLA Ops:
  6.5 212.2 %all-gather.4.cloned.1.call-start = ((), (), s32[]{:S(2)}) async-start(), calls=%async_computation.2 | async-start | bytes 11796480 | tf_op jit(solution)/shard_map/all_gather | solution.py:32
  9.0 420.0 %reduce-scatter.2.cloned.1.call-start = ((), (), s32[]{:S(2)}) async-start(), calls=%async_computation.3 | async-start | bytes 1638400 | tf_op jit(solution)/shard_map/reduce_scatter | solution.py:38
  21.1 183.7 %collective-permute-start = (f32[512,4096]{1,0:T(8,128)}, f32[512,4096]{1,0:T(8,128)}, u32[]{:S(2)}, u32[]{:S(2)}) collective-permute-start(f32[512,4096]{1,0:T(8,128)} %reduce_sum.46), channel_id=1, source_target_pairs={{0,8},{8,0},{16,24},{24,16},{1,9},{9,1},{17,25},{25,17},{2,10},{10... | collective-permute-start | bytes 25165832 | tf_op jit(solution)/shard_map/ppermute | solution.py:37
  216.0 383.7 %collective-permute-start.1 = (f32[512,4096]{1,0:T(8,128)}, f32[512,4096]{1,0:T(8,128)}, u32[]{:S(2)}, u32[]{:S(2)}) collective-permute-start(f32[512,4096]{1,0:T(8,128)} %add.22), channel_id=1, source_target_pairs={{0,16},{8,24},{16,0},{24,8},{1,17},{9,25},{17,1},{25,9},{2,18},{10... | collective-permute-start | bytes 25165832 | tf_op jit(solution)/shard_map/ppermute | solution.py:37
  240.1 370.9 %all-gather.6.cloned.1.call-start = ((), (), s32[]{:S(2)}) async-start(), calls=%async_computation.4 | async-start | bytes 2949120 | tf_op jit(solution)/shard_map/all_gather | solution.py:42
  429.0 182.0 %copy-start = (f32[512,160]{0,1:T(8,128)S(1)}, f32[512,160]{0,1:T(8,128)}, u32[]{:S(2)}) copy-start(f32[512,160]{0,1:T(8,128)} %reduce-scatter.2.cloned.1.call-done) | copy-start | bytes 983044
  429.0 250.4 %all-gather.8.cloned.1.call-start = ((), (), s32[]{:S(2)}) async-start(), calls=%async_computation.5 | async-start | bytes 2949120 | tf_op jit(solution)/shard_map/all_gather | solution.py:42
  649.0 56.7 %copy-start.1 = (f32[512,160]{0,1:T(8,128)S(1)}, f32[512,160]{0,1:T(8,128)}, u32[]{:S(2)}) copy-start(f32[512,160]{0,1:T(8,128)} %multiply_add_fusion) | copy-start | bytes 983044
Sparse Core Ops, SparseCore 0:
  9.2 67.8 all-gather.3
  240.2 188.6 reduce-scatter.1
  430.9 32.6 all-gather.5
  649.2 30.1 all-gather.7
